TPU v7x, 64 devices: a 2x2x8 block of a 4x4x8 slice. The times are simulated.
64 devices in a mesh: rep: 4 (over x, y), grp: 16 (over z, core).
Axes of the slice: x: 2, y: 2, z: 8, core: 2. Of those that a mesh axis runs over, the one named last changes fastest.
The devices are a block of a 4x4x8 slice.
Arguments:
- x_in: bfloat16 [2048, 4096], P(('rep', 'grp')), parts along dimension 0
- seq_len: int32 [2048], P(('rep', 'grp')), parts along dimension 0
- k_cache: bfloat16 [2048, 256, 2, 128], P(('rep', 'grp')), parts along dimension 0
- v_cache: bfloat16 [2048, 256, 2, 128], P(('rep', 'grp')), parts along dimension 0
- gamma_attn: bfloat16 [4096], replicated
- w_qkv: bfloat16 [4096, 4608], replicated
- b_qkv: bfloat16 [4608], replicated
- w_proj: bfloat16 [4096, 4096], replicated
- gamma_mlp: bfloat16 [4096], replicated
- w_in: bfloat16 [2, 13696, 4096], P(None, 'grp')
- w_out: bfloat16 [13696, 4096], P('grp')
Outputs:
- output 1: bfloat16 [2048, 4096], P(('rep', 'grp')), parts along dimension 0
- output 2: bfloat16 [2048, 256, 2, 128], P(('rep', 'grp')), parts along dimension 0
- output 3: bfloat16 [2048, 256, 2, 128], P(('rep', 'grp')), parts along dimension 0
There are 4 independent parts. A program takes and returns all parts, laid end to end along the dimension named above; an argument that names none is the same for every part.
All inputs are finite; a program needn't handle non-finite values.
Results may differ from a plain program's by a relative error of at most 0.0102376.
Values are sent between devices in bfloat16 or wider.
A program may use at most 768 MiB of HBM per device.

v0:
```python
import jax
import jax.numpy as jnp
from jax import lax
from jax.sharding import PartitionSpec as P

HEAD_DIM = 128
ROPE_BASE = 10000.0
EPS = 1e-5


def rms_norm(vals, gain):
    mean_sq = jnp.mean(vals * vals, axis=-1, keepdims=True)
    return (vals * lax.rsqrt(mean_sq + EPS) * gain.astype(jnp.float32)).astype(jnp.bfloat16)


def rotary(vals, positions):
    rot_dim = HEAD_DIM // 2
    inv_freq = ROPE_BASE ** (-jnp.arange(0, rot_dim, 2, dtype=jnp.float32) / rot_dim)
    angles = positions.astype(jnp.float32)[:, None] * inv_freq[None, :]
    cosine = jnp.cos(angles)[:, None, :]
    sine = jnp.sin(angles)[:, None, :]
    pairs = vals[..., :rot_dim].reshape(vals.shape[:-1] + (rot_dim // 2, 2))
    even_part = pairs[..., 0]
    odd_part = pairs[..., 1]
    rotated = jnp.stack([even_part * cosine - odd_part * sine, odd_part * cosine + even_part * sine], axis=-1)
    return jnp.concatenate([rotated.reshape(vals.shape[:-1] + (rot_dim,)), vals[..., rot_dim:]], axis=-1)


def attention_block(x_in, seq_len, k_cache, v_cache, gamma_attn, w_qkv, b_qkv, w_proj):
    batch_rows, cache_len, kv_heads = k_cache.shape[0], k_cache.shape[1], k_cache.shape[2]
    num_heads = w_proj.shape[0] // HEAD_DIM
    q_width = num_heads * HEAD_DIM
    kv_width = kv_heads * HEAD_DIM
    x_f32 = x_in.astype(jnp.float32)
    normed = rms_norm(x_f32, gamma_attn)
    qkv_proj = jnp.dot(normed, w_qkv, preferred_element_type=jnp.float32) + b_qkv.astype(jnp.float32)
    query_rot = rotary(qkv_proj[:, :q_width].reshape(batch_rows, num_heads, HEAD_DIM), seq_len).astype(jnp.bfloat16)
    key_new = rotary(qkv_proj[:, q_width:q_width + kv_width].reshape(batch_rows, kv_heads, HEAD_DIM), seq_len).astype(jnp.bfloat16)
    value_new = qkv_proj[:, q_width + kv_width:].reshape(batch_rows, kv_heads, HEAD_DIM).astype(jnp.bfloat16)
    positions = jnp.arange(cache_len, dtype=jnp.int32)
    at_len = (positions[None, :] == seq_len[:, None])[:, :, None, None]
    k_out = jnp.where(at_len, key_new[:, None], k_cache)
    v_out = jnp.where(at_len, value_new[:, None], v_cache)
    q_grouped = query_rot.reshape(batch_rows, kv_heads, num_heads // kv_heads, HEAD_DIM)
    attn_scores = jnp.einsum('bgqd,blgd->bgql', q_grouped, k_out, preferred_element_type=jnp.float32) * HEAD_DIM ** -0.5
    visible = (positions[None, :] <= seq_len[:, None])[:, None, None, :]
    attn_probs = jax.nn.softmax(jnp.where(visible, attn_scores, -jnp.inf), axis=-1).astype(jnp.bfloat16)
    context = jnp.einsum('bgql,blgd->bgqd', attn_probs, v_out, preferred_element_type=jnp.float32)
    context = context.astype(jnp.bfloat16).reshape(batch_rows, q_width)
    hidden = x_f32 + jnp.dot(context, w_proj, preferred_element_type=jnp.float32)
    return hidden, k_out, v_out


def solution(mesh):
    row_spec = P(('rep', 'grp'))
    repl_spec = P()

    def local_layer(x_in, seq_len, k_cache, v_cache, gamma_attn, w_qkv, b_qkv, w_proj, gamma_mlp, w_in, w_out):
        hidden, k_out, v_out = attention_block(x_in, seq_len, k_cache, v_cache, gamma_attn, w_qkv, b_qkv, w_proj)
        mlp_in = rms_norm(hidden, gamma_mlp)
        group_rows = lax.all_gather(mlp_in, 'grp', axis=0, tiled=True)
        gate_up = jnp.einsum('bh,cfh->bcf', group_rows, w_in, preferred_element_type=jnp.float32)
        swiglu = (jax.nn.silu(gate_up[:, 0]) * gate_up[:, 1]).astype(jnp.bfloat16)
        part_sum = jnp.dot(swiglu, w_out, preferred_element_type=jnp.float32).astype(jnp.bfloat16)
        mlp_out = lax.psum_scatter(part_sum, 'grp', scatter_dimension=0, tiled=True)
        layer_out = (hidden + mlp_out.astype(jnp.float32)).astype(jnp.bfloat16)
        return layer_out, k_out, v_out

    return jax.shard_map(local_layer, mesh=mesh,
                         in_specs=(row_spec, row_spec, row_spec, row_spec, repl_spec, repl_spec, repl_spec,
                                   repl_spec, repl_spec, P(None, 'grp', None), P('grp', None)),
                         out_specs=(row_spec, row_spec, row_spec), check_vma=False)
```

profile of v0, /device:TPU:22, one launch (start us, length us, event | category | flops | bytes accessed | tf_op | source)
XLA Modules:
  0.0 195.6 jit_solution(11582038698554048172)
XLA Ops:
  7.3 0.7 convert_element_type.59
  7.9 0.7 iota_compare_fusion.1
  8.7 1.1 fusion.22
  9.8 0.7 convert_element_type.56
  10.5 0.7 convert_element_type.58
  11.2 15.2 %convolution_add_fusion = f32[32,4608]{1,0:T(8,128)S(1)} fusion(bf16[4096,4608]{1,0:T(8,128)(2,1)} %param.16, f32[4608]{0:T(1024)S(1)} %convert_element_type.58, bf16[32,4096]{1,0:T(8,128)(2,1)} %param.11, f32[4096]{0:T(1024)S(1)} %convert_element_type.56, f32[32]{0:T(128)S(1)} %add_rsqrt_fusion.1), kind=kOutput, calls=%fused_computation.4 | convolution fusion | flops 1208631296 | bytes 38635648 | tf_op jit(solution)/shard_map/dot_general | solution.py:36
  26.9 0.1 multiply_cosine_fusion
  27.4 0.1 slice.89
  27.6 0.9 copy.58
  28.5 0.3 subtract_convert_fusion
  28.8 0.1 pad_maximum_fusion
  28.9 0.3 copy.50
  29.2 0.8 copy.51
  30.0 13.7 %broadcast_select_fusion.1 = (bf16[32,256,2,128]{3,2,1,0:T(2,128)(2,1)}, bf16[32,256,2,128]{3,2,1,0:T(2,128)(2,1)}) fusion(bf16[32,256,2,128]{3,2,1,0:T(2,128)(2,1)} %param.13, pred[32,256]{1,0:T(8,128)(4,1)S(1)} %get-tuple-element.12, bf16[32,2,128]{2,1,0:T(2,128)(2,1)S(1)} %copy.55, bf16[32,256,2,128]{3,2,1,0:T(2,128)(2,1)} %param.14, ...), kind=kLoop, calls=%fused_computation.2 | loop fusion | flops 4194304 | bytes 16818176 | tf_op jit(solution)/shard_map/jit(_where)/select_n | solution.py:42
  43.7 3.6 %fusion.36 = (f32[32,2,16]{2,1,0:T(2,128)S(1)}, f32[32,2,16,256]{3,2,1,0:T(8,128)S(1)}) fusion(bf16[32,256,2,128]{3,2,1,0:T(2,128)(2,1)} %get-tuple-element.7, pred[32,256]{1,0:T(8,128)(4,1)S(1)} %get-tuple-element.11, bf16[32,2,16,64]{3,2,1,0:T(8,128)(2,1)S(1)} %bitcast.43, bf16[32,2,16,64]{3,2,1,0:T(8,128)(2,1)S(1)} %copy.51), kind=kOutput, calls=%fused_computation.59 | convolution fusion | flops 68681984 | bytes 5517312 | tf_op jit(solution)/shard_map/sub | solution.py:47
  47.4 2.9 %fusion.17 = bf16[32,2,16,128]{3,2,1,0:T(8,128)(2,1)S(1)} fusion(bf16[32,256,2,128]{3,2,1,0:T(2,128)(2,1)} %get-tuple-element.8, f32[32,2,16,256]{3,2,1,0:T(8,128)S(1)} %get-tuple-element.14, f32[32,2,16]{2,1,0:T(2,128)S(1)} %get-tuple-element.13), kind=kOutput, calls=%fused_computation.20 | convolution fusion | flops 67764224 | bytes 5509120 | tf_op jit(solution)/shard_map/bgql,blgd->bgqd/dot_general | solution.py:48
  50.3 13.7 %multiply_reduce_fusion = (f32[32]{0:T(128)S(1)}, f32[32,4096]{1,0:T(8,128)S(1)}) fusion(bf16[4096,4096]{1,0:T(8,128)(2,1)} %param.18, bf16[4,8,32,128]{3,2,1,0:T(8,128)(2,1)S(1)} %bitcast.42, bf16[32,4096]{1,0:T(8,128)(2,1)S(1)} %copy-done), kind=kOutput, calls=%fused_computation.33 | convolution fusion | flops 1074266112 | bytes 34603136 | tf_op jit(solution)/shard_map/dot_general | solution.py:50
  64.0 0.8 multiply_convert_fusion
  64.9 0.2 reduce-scatter.2.cloned.1.call-start
  65.1 42.3 %all-gather.2.cloned.1.call-done = bf16[512,4096]{1,0:T(8,128)(2,1)} async-done(((bf16[32,4096]{1,0:T(8,128)(2,1)}), bf16[512,4096]{1,0:T(8,128)(2,1)}) %all-gather.2.cloned.1.call-update) | async-done | bytes 4194320 | tf_op jit(solution)/shard_map/all_gather | solution.py:61
  107.4 11.7 %fusion.1 = f32[512,2,856]{0,2,1:T(8,128)S(1)} fusion(bf16[2,856,4096]{2,1,0:T(8,128)(2,1)} %param.20, bf16[512,4096]{1,0:T(8,128)(2,1)} %all-gather.2.cloned.1.call-done), kind=kOutput, calls=%fused_computation.6 | convolution fusion | flops 7180648448 | bytes 21725184 | tf_op jit(solution)/shard_map/bh,cfh->bcf/dot_general | solution.py:62
  119.1 9.5 %convolution_convert_fusion = bf16[512,4096]{1,0:T(8,128)(2,1)} fusion(bf16[856,4096]{1,0:T(8,128)(2,1)} %param.21, f32[512,2,856]{0,2,1:T(8,128)S(1)} %fusion.1), kind=kOutput, calls=%fused_computation.3 | convolution fusion | flops 3595051008 | bytes 14712832 | tf_op jit(solution)/shard_map/dot_general | solution.py:64
  128.7 58.3 %reduce-scatter.2.cloned.1.call-done = bf16[32,4096]{1,0:T(8,128)(2,1)} async-done(((bf16[512,4096]{1,0:T(8,128)(2,1)}), bf16[32,4096]{1,0:T(8,128)(2,1)}) %reduce-scatter.2.cloned.1.call-update) | async-done | bytes 262160 | tf_op jit(solution)/shard_map/reduce_scatter | solution.py:65
  187.0 1.7 add_convert_fusion
  (25 shorter events, 0.9 us)
Async XLA Ops:
  7.2 100.2 %all-gather.2.cloned.1.call-start = ((), (), s32[]{:S(2)}) async-start(), calls=%async_computation.1 | async-start | bytes 4456448 | tf_op jit(solution)/shard_map/all_gather | solution.py:61
  11.2 15.3 %copy-start.1 = (bf16[4096]{0:T(1024)(128)(2,1)S(1)}, bf16[4096]{0:T(1024)(128)(2,1)}, u32[]{:S(2)}) copy-start(bf16[4096]{0:T(1024)(128)(2,1)} %param.19) | copy-start | bytes 24580
  47.3 3.0 %copy-start = (bf16[32,4096]{1,0:T(8,128)(2,1)S(1)}, bf16[32,4096]{1,0:T(8,128)(2,1)}, u32[]{:S(2)}) copy-start(bf16[32,4096]{1,0:T(8,128)(2,1)} %param.11) | copy-start | bytes 786436
  64.9 122.1 %reduce-scatter.2.cloned.1.call-start = ((), (), s32[]{:S(2)}) async-start(), calls=%async_computation.2 | async-start | bytes 4456448 | tf_op jit(solution)/shard_map/reduce_scatter | solution.py:65
Sparse Core Ops, SparseCore 0:
  65.0 42.3 all-gather.1
  128.8 58.1 reduce-scatter.1
where the time goes:
time: 196 us
  waiting for transfers between devices  101 us (52%)
  matrix products  56.7 us (29%)
  other arithmetic  21 us (11%)
  between operations  14.3 us (7%)
  local copies, waits for them, and re-layouts  2.58 us (1%)
    reduce_scatter x1, waiting for transfers between devices, local_layer(): mlp_out = lax.psum_scatter(part_sum, 'grp', scatter_dimension=0, tiled=True)  58.3 us
    all_gather x1, waiting for transfers between devices, local_layer(): group_rows = lax.all_gather(mlp_in, 'grp', axis=0, tiled=True)  42.3 us
    dot_general x1, matrix products, attention_block(): jnp.dot(normed, w_qkv, preferred_element_type=jnp.float32)  15.2 us
    select_n x1, other arithmetic, attention_block(): k_out = jnp.where(at_len, key_new[:, None], k_cache)  13.7 us
    dot_general x1, matrix products, attention_block(): jnp.dot(context, w_proj, preferred_element_type=jnp.float32)  13.7 us
    dot_general x1, matrix products, local_layer(): jnp.einsum('bh,cfh->bcf', group_rows, w_in, preferred_element_type=jnp.fl...  11.7 us
    dot_general x1, matrix products, local_layer(): jnp.dot(swiglu, w_out, preferred_element_type=jnp.float32)  9.53 us
  transfers between devices with their start and end apart: 2, of which 2 were waited for; matrix products, arithmetic and copies ran while one was open for 0% of the time, Pallas kernels for 0%

commit v1 on v0

--- a/solution.py
+++ b/solution.py
@@ -1,11 +1,17 @@
+import functools
+
 import jax
 import jax.numpy as jnp
 from jax import lax
+from jax.experimental import pallas as pl
+from jax.experimental.pallas import tpu as pltpu
 from jax.sharding import PartitionSpec as P
 
 HEAD_DIM = 128
 ROPE_BASE = 10000.0
 EPS = 1e-5
+MESH = pl.DeviceIdType.MESH
+LANES = 128
 
 
 def rms_norm(vals, gain):
@@ -51,6 +57,240 @@
     return hidden, k_out, v_out
 
 
+def mlp_kernel(chips, m_ref, h_ref, w_in_ref, w_out_ref, o_ref, m_all, w1, w2, act, part, pair_rx, rs_rx, rs_tx,
+               w1_sem, w2_sem, ag_send, ag_recv, pt_send, pt_recv, px_send, px_recv, rs_send, rs_recv):
+    f32, bf16 = jnp.float32, jnp.bfloat16
+    width = m_ref.shape[1]
+    half = width // 2
+    rb = m_ref.shape[0] // 2
+    ffn = w_out_ref.shape[0]
+    fblocks = w2.shape[0] // LANES
+    far = chips // 2
+    ncol = 512
+
+    me = lax.axis_index('grp')
+    z, core = me // 2, me % 2
+    other = 1 - core
+    right = lax.rem(z + 1, chips) * 2 + core
+    left = lax.rem(z + chips - 1, chips) * 2 + core
+    partner = z * 2 + other
+    nbr = (right, left)
+
+    def chip_at(direction, k):
+        return lax.rem(z + (chips - k if direction == 0 else k), chips)
+
+    def rows(c, chip):
+        return pl.ds(pl.multiple_of((c * chips + chip) * rb, rb), rb)
+
+    def rcopy(src, dst, ssem, rsem, dev):
+        return pltpu.make_async_remote_copy(src_ref=src, dst_ref=dst, send_sem=ssem, recv_sem=rsem,
+                                            device_id={'grp': dev}, device_id_type=MESH)
+
+    w_copies = []
+    for j in range(fblocks):
+        n = min(LANES, ffn - j * LANES)
+        for c in range(2):
+            w_copies.append(pltpu.make_async_copy(w_in_ref.at[c, pl.ds(j * LANES, n), :],
+                                                  w1.at[pl.ds((2 * j + c) * LANES, n), :], w1_sem.at[2 * j + c]))
+    w_copies.append(pltpu.make_async_copy(w_out_ref, w2.at[pl.ds(0, ffn), :], w2_sem))
+
+    barrier = pltpu.get_barrier_semaphore()
+    for dev in (right, left, partner):
+        pl.semaphore_signal(barrier, inc=1, device_id={'grp': dev}, device_id_type=MESH)
+    pl.semaphore_wait(barrier, 3)
+
+    def ag_cols(direction, k):
+        return pl.ds(direction * half, half) if k == far else pl.ds(0, width)
+
+    def ag(b, direction, k):
+        cols = ag_cols(direction, k)
+        if k == 1:
+            src = m_ref.at[pl.ds(b * rb, rb), :]
+            sent = z
+        else:
+            sent = chip_at(direction, k - 1)
+            src = m_all.at[b, rows(core, sent), cols]
+        return rcopy(src, m_all.at[b, rows(core, sent), cols], ag_send.at[b, direction, k - 1],
+                     ag_recv.at[b, direction, k - 1], nbr[direction])
+
+    def ag_wait(b, direction, k):
+        got = m_all.at[b, rows(core, chip_at(direction, k)), ag_cols(direction, k)]
+        rcopy(got, got, ag_send.at[b, direction, k - 1], ag_recv.at[b, direction, k - 1], nbr[direction]).wait_recv()
+
+    def pt(b, direction, k):
+        if k == 0:
+            blk = m_all.at[b, rows(core, z), :]
+            return rcopy(m_ref.at[pl.ds(b * rb, rb), :], blk, pt_send.at[b, 0], pt_recv.at[b, 0], partner)
+        slot = 1 + direction * far + k - 1
+        blk = m_all.at[b, rows(core, chip_at(direction, k)), ag_cols(direction, k)]
+        return rcopy(blk, blk, pt_send.at[b, slot], pt_recv.at[b, slot], partner)
+
+    def pt_wait(b, direction, k):
+        if k == 0:
+            blk = m_all.at[b, rows(other, z), :]
+            return rcopy(blk, blk, pt_send.at[b, 0], pt_recv.at[b, 0], partner).wait_recv()
+        slot = 1 + direction * far + k - 1
+        blk = m_all.at[b, rows(other, chip_at(direction, k)), ag_cols(direction, k)]
+        return rcopy(blk, blk, pt_send.at[b, slot], pt_recv.at[b, slot], partner).wait_recv()
+
+    started = []
+
+    def start(copy):
+        copy.start()
+        started.append(copy)
+
+    for b in range(2):
+        for d in range(2):
+            start(ag(b, d, 1))
+    for b in range(2):
+        start(pt(b, 0, 0))
+    for copy in w_copies:
+        copy.start()
+    for b in range(2):
+        m_all[b, rows(core, z), :] = m_ref[pl.ds(b * rb, rb), :]
+    for k in range(1, far + 1):
+        for b in range(2):
+            for d in range(2):
+                ag_wait(b, d, k)
+                if k < far:
+                    start(ag(b, d, k + 1))
+                start(pt(b, d, k))
+    for copy in w_copies:
+        copy.wait()
+    edge = ffn // 16 * 16
+    if edge < w2.shape[0]:
+        tail = w2[pl.ds(edge, w2.shape[0] - edge), :]
+        row = lax.broadcasted_iota(jnp.int32, tail.shape, 0)
+        w2[pl.ds(edge, w2.shape[0] - edge), :] = jnp.where(row < ffn - edge, tail.astype(f32), 0.0).astype(bf16)
+
+    def gather_wait(b):
+        pt_wait(b, 0, 0)
+        for k in range(1, far + 1):
+            for d in range(2):
+                pt_wait(b, d, k)
+
+    def up(b, lo, hi):
+        def body(j, carry):
+            wj = w1[pl.ds(pl.multiple_of(j * 2 * LANES, 2 * LANES), 2 * LANES), :]
+            gu = lax.dot_general(m_all[b], wj, (((1,), (1,)), ((), ())), preferred_element_type=f32)
+            gate, upv = gu[:, :LANES], gu[:, LANES:]
+            val = gate / (1.0 + jnp.exp(-gate)) * upv
+            col = lax.broadcasted_iota(jnp.int32, val.shape, 1) + j * LANES
+            act[:, pl.ds(pl.multiple_of(j * LANES, LANES), LANES)] = jnp.where(col < ffn, val, 0.0).astype(bf16)
+            return carry
+        lax.fori_loop(lo, hi, body, 0)
+
+    def px(b, n):
+        cols = pl.ds(n * ncol if isinstance(n, int) else pl.multiple_of(n * ncol, ncol), ncol)
+        src = part.at[b, pl.ds(pl.multiple_of(other * chips * rb, chips * rb), chips * rb), cols]
+        return rcopy(src, pair_rx.at[b, :, cols], px_send.at[b, n], px_recv.at[b, n], partner)
+
+    def down(b, lo, hi):
+        def body(n, carry):
+            cols = pl.ds(pl.multiple_of(n * ncol, ncol), ncol)
+            part[b, :, cols] = jnp.dot(act[...], w2[:, cols], preferred_element_type=f32).astype(bf16)
+            px(b, n).start()
+            return carry
+        lax.fori_loop(lo, hi, body, 0)
+
+    def pair_sum(b, chip, cols):
+        mine = part[b, rows(core, chip), cols].astype(f32)
+        return mine + pair_rx[b, pl.ds(pl.multiple_of(chip * rb, rb), rb), cols].astype(f32)
+
+    def rs(b, direction, left_hops, hf):
+        cols = pl.ds(hf * half, half)
+        return rcopy(rs_tx.at[b, direction, left_hops, :, cols], rs_rx.at[b, direction, left_hops, :, cols],
+                     rs_send.at[b, direction, left_hops, hf], rs_recv.at[b, direction, left_hops, hf], nbr[direction])
+
+    def rs_step(b, k):
+        for hf in range(2):
+            cols = pl.ds(hf * half, half)
+            for d in range(2):
+                if k == far and hf != d:
+                    continue
+                val = pair_sum(b, chip_at(1 - d, k), cols)
+                if k < far and (k < far - 1 or hf == d):
+                    rs(b, d, k, hf).wait_recv()
+                    val = val + rs_rx[b, d, k, :, cols].astype(f32)
+                rs_tx[b, d, k - 1, :, cols] = val.astype(bf16)
+                start(rs(b, d, k - 1, hf))
+
+    def rs_last(b):
+        for hf in range(2):
+            cols = pl.ds(hf * half, half)
+            val = pair_sum(b, z, cols)
+            for d in range(2):
+                rs(b, d, 0, hf).wait_recv()
+                val = val + rs_rx[b, d, 0, :, cols].astype(f32)
+            o_ref[pl.ds(b * rb, rb), cols] = (h_ref[pl.ds(b * rb, rb), cols] + val).astype(bf16)
+
+    nblk = width // ncol
+
+    def pair_wait(b):
+        for n in range(nblk):
+            px(b, n).wait()
+
+    gather_wait(0)
+    up(0, 0, fblocks)
+    down(0, 0, nblk)
+    gather_wait(1)
+    pair_wait(0)
+    rs_step(0, far)
+    cuts = [i * fblocks // 2 for i in range(3)]
+    up(1, cuts[0], cuts[1])
+    rs_step(0, 3) if far > 3 else None
+    up(1, cuts[1], cuts[2])
+    rs_step(0, 2)
+    down(1, 0, nblk)
+    pair_wait(1)
+    rs_step(1, far)
+    rs_step(0, 1)
+    rs_step(1, 3) if far > 3 else None
+    rs_last(0)
+    rs_step(1, 2)
+    rs_step(1, 1)
+    rs_last(1)
+    for copy in started:
+        copy.wait_send()
+
+
+def mlp_layer(mesh, hidden, mlp_in, w_in, w_out):
+    rows, width = mlp_in.shape
+    group = mesh.shape['grp']
+    chips = group // 2
+    far = chips // 2
+    rb = rows // 2
+    ffn = w_out.shape[0]
+    fpad = -(-ffn // LANES) * LANES
+    bf16 = jnp.bfloat16
+    vmem = pl.BlockSpec(memory_space=pltpu.VMEM)
+    hbm = pl.BlockSpec(memory_space=pl.ANY)
+    dma = pltpu.SemaphoreType.DMA
+    return pl.pallas_call(
+        functools.partial(mlp_kernel, chips),
+        name='mlp_ring',
+        out_shape=jax.ShapeDtypeStruct((rows, width), bf16),
+        in_specs=[vmem, vmem, hbm, hbm],
+        out_specs=vmem,
+        scratch_shapes=[
+            pltpu.VMEM((2, group * rb, width), bf16),
+            pltpu.VMEM((2 * fpad, width), bf16),
+            pltpu.VMEM((fpad, width), bf16),
+            pltpu.VMEM((group * rb, fpad), bf16),
+            pltpu.VMEM((2, group * rb, width), bf16),
+            pltpu.VMEM((2, chips * rb, width), bf16),
+            pltpu.VMEM((2, 2, far, rb, width), bf16),
+            pltpu.VMEM((2, 2, far, rb, width), bf16),
+            dma((2 * fpad // LANES,)), dma,
+            dma((2, 2, far)), dma((2, 2, far)),
+            dma((2, 2 * far + 1)), dma((2, 2 * far + 1)),
+            dma((2, width // 512)), dma((2, width // 512)),
+            dma((2, 2, far, 2)), dma((2, 2, far, 2)),
+        ],
+        compiler_params=pltpu.CompilerParams(collective_id=0, has_side_effects=True, vmem_limit_bytes=60 * 1024 * 1024),
+    )(mlp_in, hidden, w_in, w_out)
+
+
 def solution(mesh):
     row_spec = P(('rep', 'grp'))
     repl_spec = P()
@@ -58,12 +298,7 @@
     def local_layer(x_in, seq_len, k_cache, v_cache, gamma_attn, w_qkv, b_qkv, w_proj, gamma_mlp, w_in, w_out):
         hidden, k_out, v_out = attention_block(x_in, seq_len, k_cache, v_cache, gamma_attn, w_qkv, b_qkv, w_proj)
         mlp_in = rms_norm(hidden, gamma_mlp)
-        group_rows = lax.all_gather(mlp_in, 'grp', axis=0, tiled=True)
-        gate_up = jnp.einsum('bh,cfh->bcf', group_rows, w_in, preferred_element_type=jnp.float32)
-        swiglu = (jax.nn.silu(gate_up[:, 0]) * gate_up[:, 1]).astype(jnp.bfloat16)
-        part_sum = jnp.dot(swiglu, w_out, preferred_element_type=jnp.float32).astype(jnp.bfloat16)
-        mlp_out = lax.psum_scatter(part_sum, 'grp', scatter_dimension=0, tiled=True)
-        layer_out = (hidden + mlp_out.astype(jnp.float32)).astype(jnp.bfloat16)
+        layer_out = mlp_layer(mesh, hidden, mlp_in, w_in, w_out)
         return layer_out, k_out, v_out
 
     return jax.shard_map(local_layer, mesh=mesh,

time: 196 us -> 136 us (0.69)
  waiting for transfers between devices: 101 us -> 0 us
  Pallas kernels: 0 us -> 75.1 us
  matrix products: 56.7 us -> 35.5 us
  between operations: 14.3 us -> 0.82 us
    pallas_call x0 -> x1, Pallas kernels: none -> 75.1 us  [mlp_layer(): pl.pallas_call(functools.partial(mlp_kernel, chips), name='mlp_ring', out...]
    reduce_scatter x1 -> x0, waiting for transfers between devices: 58.3 us -> none  [local_layer(): mlp_out = lax.psum_scatter(part_sum, 'grp', scatter_dimension=0, tiled=True)]
    all_gather x1 -> x0, waiting for transfers between devices: 42.3 us -> none  [local_layer(): group_rows = lax.all_gather(mlp_in, 'grp', axis=0, tiled=True)]
    dot_general x2 -> x0, matrix products: 21.2 us -> none  [the longest x1 11.7 us: local_layer(): jnp.einsum('bh,cfh->bcf', group_rows, w_in, preferred_element_type=jnp.fl...]
  transfers between devices with their start and end apart: 2 -> 0, of which waited for: 2 -> 0; matrix products, arithmetic and copies ran while one was open for 0% -> 0% of each run, Pallas kernels for 0% -> 0%
where the time goes in v1:
time: 136 us
  Pallas kernels  75.1 us (55%)
  matrix products  35.5 us (26%)
  other arithmetic  20.1 us (15%)
  local copies, waits for them, and re-layouts  4.25 us (3%)
    pallas_call x1, Pallas kernels, mlp_layer(): pl.pallas_call(functools.partial(mlp_kernel, chips), name='mlp_ring', out...  75.1 us
    dot_general x1, matrix products, attention_block(): jnp.dot(normed, w_qkv, preferred_element_type=jnp.float32)  15.2 us
    select_n x1, other arithmetic, attention_block(): k_out = jnp.where(at_len, key_new[:, None], k_cache)  13.7 us
    dot_general x1, matrix products, attention_block(): jnp.dot(context, w_proj, preferred_element_type=jnp.float32)  13.7 us
    sub x1, matrix products, attention_block(): jax.nn.softmax(jnp.where(visible, attn_scores, -jnp.inf), axis=-1)  3.62 us
    dot_general x1, matrix products, attention_block(): jnp.einsum('bgql,blgd->bgqd', attn_probs, v_out, preferred_element_type=j...  2.94 us
    unnamed x9, local copies, waits for them, and re-layouts  2.74 us

profile of v1, /device:TPU:22, one launch (start us, length us, event | category | flops | bytes accessed | tf_op | source)
XLA Modules:
  0.0 135.7 jit_solution(7189823209886191812)
XLA Ops:
  0.6 0.7 convert_element_type.47
  1.3 1.1 fusion.16
  2.4 0.7 convert_element_type.44
  3.1 0.7 convert_element_type.51
  3.8 0.7 iota_compare_fusion.1
  4.6 0.7 convert_element_type.46
  5.3 0.1 multiply_cosine_fusion
  5.4 15.2 %convolution_add_fusion = f32[32,4608]{1,0:T(8,128)S(1)} fusion(bf16[4096,4608]{1,0:T(8,128)(2,1)} %param.16, f32[4608]{0:T(1024)S(1)} %convert_element_type.46, bf16[32,4096]{1,0:T(8,128)(2,1)} %param.11, f32[4096]{0:T(1024)S(1)} %convert_element_type.44, f32[32]{0:T(128)S(1)} %add_rsqrt_fusion.1), kind=kOutput, calls=%fused_computation.3 | convolution fusion | flops 1208631296 | bytes 38635648 | tf_op jit(solution)/shard_map/dot_general | solution.py:42
  20.8 0.1 copy.61
  21.1 0.1 subtract_convert_fusion.1
  21.2 0.1 pad_maximum_fusion.1
  21.5 0.1 slice.69
  21.6 0.9 copy.58
  22.6 0.3 subtract_convert_fusion
  22.9 0.1 pad_maximum_fusion
  23.0 0.3 copy.50
  23.3 0.8 copy.51
  24.1 13.7 %broadcast_select_fusion.1 = (bf16[32,256,2,128]{3,2,1,0:T(2,128)(2,1)}, bf16[32,256,2,128]{3,2,1,0:T(2,128)(2,1)}) fusion(bf16[32,256,2,128]{3,2,1,0:T(2,128)(2,1)} %param.13, pred[32,256]{1,0:T(8,128)(4,1)S(1)} %get-tuple-element.12, bf16[32,2,128]{2,1,0:T(2,128)(2,1)S(1)} %copy.55, bf16[32,256,2,128]{3,2,1,0:T(2,128)(2,1)} %param.14, ...), kind=kLoop, calls=%fused_computation.2 | loop fusion | flops 4194304 | bytes 16818176 | tf_op jit(solution)/shard_map/jit(_where)/select_n | solution.py:48
  37.8 3.6 %fusion.29 = (f32[32,2,16]{2,1,0:T(2,128)S(1)}, f32[32,2,16,256]{3,2,1,0:T(8,128)S(1)}) fusion(bf16[32,256,2,128]{3,2,1,0:T(2,128)(2,1)} %get-tuple-element.21, pred[32,256]{1,0:T(8,128)(4,1)S(1)} %get-tuple-element.11, bf16[32,2,16,64]{3,2,1,0:T(8,128)(2,1)S(1)} %bitcast.26, bf16[32,2,16,64]{3,2,1,0:T(8,128)(2,1)S(1)} %copy.51), kind=kOutput, calls=%fused_computation.49 | convolution fusion | flops 68681984 | bytes 5517312 | tf_op jit(solution)/shard_map/sub | solution.py:53
  41.4 2.9 %fusion.13 = bf16[32,2,16,128]{3,2,1,0:T(8,128)(2,1)S(1)} fusion(bf16[32,256,2,128]{3,2,1,0:T(2,128)(2,1)} %get-tuple-element.22, f32[32,2,16,256]{3,2,1,0:T(8,128)S(1)} %get-tuple-element.14, f32[32,2,16]{2,1,0:T(2,128)S(1)} %get-tuple-element.13), kind=kOutput, calls=%fused_computation.13 | convolution fusion | flops 67764224 | bytes 5509120 | tf_op jit(solution)/shard_map/bgql,blgd->bgqd/dot_general | solution.py:54
  44.4 13.7 %multiply_reduce_fusion = (f32[32]{0:T(128)S(1)}, f32[32,4096]{1,0:T(8,128)S(1)}) fusion(bf16[4096,4096]{1,0:T(8,128)(2,1)} %param.18, bf16[4,8,32,128]{3,2,1,0:T(8,128)(2,1)S(1)} %bitcast.25, bf16[32,4096]{1,0:T(8,128)(2,1)S(1)} %copy-done.1), kind=kOutput, calls=%fused_computation.24 | convolution fusion | flops 1074266112 | bytes 34603136 | tf_op jit(solution)/shard_map/dot_general | solution.py:56
  58.1 0.9 multiply_convert_fusion.m_ref
  58.9 75.1 %mlp_ring.1 = bf16[32,4096]{1,0:T(8,128)(2,1)} custom-call(bf16[32,4096]{1,0:T(8,128)(2,1)} %multiply_convert_fusion.m_ref, f32[32,4096]{1,0:T(8,128)} %copy-done, bf16[2,856,4096]{2,1,0:T(8,128)(2,1)} %w_in_ref.1, bf16[856,4096]{1,0:T(8,128)(2,1)} %w_out_ref.1), custom_call_target="tpu_custom_call" | custom-call | tf_op jit(solution)/shard_map/mlp_ring/pallas_call | solution.py:269
  134.0 1.7 %copy.84 = bf16[32,4096]{1,0:T(8,128)(2,1)} copy(bf16[32,4096]{1,0:T(8,128)(2,1)} %mlp_ring.1) | data formatting | bytes 524288
  (18 shorter events, 0.5 us)
Async XLA Ops:
  41.4 3.0 %copy-start.1 = (bf16[32,4096]{1,0:T(8,128)(2,1)S(1)}, bf16[32,4096]{1,0:T(8,128)(2,1)}, u32[]{:S(2)}) copy-start(bf16[32,4096]{1,0:T(8,128)(2,1)} %param.11) | copy-start | bytes 786436
  58.1 0.9 copy-start

commit v2 on v1

--- a/solution.py
+++ b/solution.py
@@ -1,4 +1,5 @@
 import functools
+import math
 
 import jax
 import jax.numpy as jnp
@@ -14,47 +15,186 @@
 LANES = 128
 
 
-def rms_norm(vals, gain):
-    mean_sq = jnp.mean(vals * vals, axis=-1, keepdims=True)
-    return (vals * lax.rsqrt(mean_sq + EPS) * gain.astype(jnp.float32)).astype(jnp.bfloat16)
-
-
-def rotary(vals, positions):
+def attn_kernel(len_ref, x_ref, ga_ref, b_ref, gm_ref, w_qkv, w_proj, k_in, v_in, h_out, m_out, k_out, v_out,
+                wbuf, kbuf, vbuf, normed, qs, cs, ctx, new, wsem, kv_sem, out_sem):
+    f32, bf16 = jnp.float32, jnp.bfloat16
+    rows, width = x_ref.shape
+    cache = kbuf.shape[1]
+    slots, _, ncol = wbuf.shape
+    heads = qs.shape[0] // rows
+    nq = w_qkv.shape[1] // ncol
+    nproj = w_proj.shape[1] // ncol
+    per = ncol // HEAD_DIM
+    nseq = 4
+
+    def weight(i, slot):
+        src = w_qkv.at[:, pl.ds(i * ncol, ncol)] if i < nq else w_proj.at[:, pl.ds((i - nq) * ncol, ncol)]
+        return pltpu.make_async_copy(src, wbuf.at[slot], wsem.at[slot])
+
+    def weight_dyn(src, i, slot):
+        return pltpu.make_async_copy(src.at[:, pl.ds(pl.multiple_of(i * ncol, ncol), ncol)], wbuf.at[slot], wsem.at[slot])
+
+    def kv(src, dst, i):
+        return pltpu.make_async_copy(src.at[pl.ds(i * 8, 8)], dst.at[pl.ds(i * 8, 8)], kv_sem.at[i])
+
+    for i in range(slots):
+        weight(i, i).start()
+
+    def normalize(vals, gain):
+        mean_sq = jnp.mean(vals * vals, axis=-1, keepdims=True)
+        return (vals * lax.rsqrt(mean_sq + EPS) * gain).astype(bf16)
+
+    normed[...] = normalize(x_ref[...].astype(f32), ga_ref[...].astype(f32))
+
+    row = lax.broadcasted_iota(jnp.int32, (rows, HEAD_DIM), 0)
+    lane = lax.broadcasted_iota(jnp.int32, (rows, HEAD_DIM), 1)
     rot_dim = HEAD_DIM // 2
-    inv_freq = ROPE_BASE ** (-jnp.arange(0, rot_dim, 2, dtype=jnp.float32) / rot_dim)
-    angles = positions.astype(jnp.float32)[:, None] * inv_freq[None, :]
-    cosine = jnp.cos(angles)[:, None, :]
-    sine = jnp.sin(angles)[:, None, :]
-    pairs = vals[..., :rot_dim].reshape(vals.shape[:-1] + (rot_dim // 2, 2))
-    even_part = pairs[..., 0]
-    odd_part = pairs[..., 1]
-    rotated = jnp.stack([even_part * cosine - odd_part * sine, odd_part * cosine + even_part * sine], axis=-1)
-    return jnp.concatenate([rotated.reshape(vals.shape[:-1] + (rot_dim,)), vals[..., rot_dim:]], axis=-1)
-
-
-def attention_block(x_in, seq_len, k_cache, v_cache, gamma_attn, w_qkv, b_qkv, w_proj):
-    batch_rows, cache_len, kv_heads = k_cache.shape[0], k_cache.shape[1], k_cache.shape[2]
-    num_heads = w_proj.shape[0] // HEAD_DIM
-    q_width = num_heads * HEAD_DIM
-    kv_width = kv_heads * HEAD_DIM
-    x_f32 = x_in.astype(jnp.float32)
-    normed = rms_norm(x_f32, gamma_attn)
-    qkv_proj = jnp.dot(normed, w_qkv, preferred_element_type=jnp.float32) + b_qkv.astype(jnp.float32)
-    query_rot = rotary(qkv_proj[:, :q_width].reshape(batch_rows, num_heads, HEAD_DIM), seq_len).astype(jnp.bfloat16)
-    key_new = rotary(qkv_proj[:, q_width:q_width + kv_width].reshape(batch_rows, kv_heads, HEAD_DIM), seq_len).astype(jnp.bfloat16)
-    value_new = qkv_proj[:, q_width + kv_width:].reshape(batch_rows, kv_heads, HEAD_DIM).astype(jnp.bfloat16)
-    positions = jnp.arange(cache_len, dtype=jnp.int32)
-    at_len = (positions[None, :] == seq_len[:, None])[:, :, None, None]
-    k_out = jnp.where(at_len, key_new[:, None], k_cache)
-    v_out = jnp.where(at_len, value_new[:, None], v_cache)
-    q_grouped = query_rot.reshape(batch_rows, kv_heads, num_heads // kv_heads, HEAD_DIM)
-    attn_scores = jnp.einsum('bgqd,blgd->bgql', q_grouped, k_out, preferred_element_type=jnp.float32) * HEAD_DIM ** -0.5
-    visible = (positions[None, :] <= seq_len[:, None])[:, None, None, :]
-    attn_probs = jax.nn.softmax(jnp.where(visible, attn_scores, -jnp.inf), axis=-1).astype(jnp.bfloat16)
-    context = jnp.einsum('bgql,blgd->bgqd', attn_probs, v_out, preferred_element_type=jnp.float32)
-    context = context.astype(jnp.bfloat16).reshape(batch_rows, q_width)
-    hidden = x_f32 + jnp.dot(context, w_proj, preferred_element_type=jnp.float32)
-    return hidden, k_out, v_out
+    pos = jnp.zeros((rows, HEAD_DIM), jnp.int32)
+    for i in range(rows):
+        pos = jnp.where(row == i, len_ref[i], pos)
+    even = lane % 2 == 0
+    freq = jnp.exp((lane // 2 * 2).astype(f32) * (-math.log(ROPE_BASE) / rot_dim))
+    angle = pos.astype(f32) * freq
+    turned = lane < rot_dim
+    cosine = jnp.where(turned, jnp.cos(angle), 1.0)
+    sine = jnp.where(turned, jnp.sin(angle), 0.0)
+    sine = jnp.where(even, -sine, sine)
+
+    def rotate(vals):
+        swapped = jnp.where(even, pltpu.roll(vals, HEAD_DIM - 1, 1), pltpu.roll(vals, 1, 1))
+        return vals * cosine + swapped * sine
+
+    def project(lhs, slot):
+        return jnp.dot(lhs[...], wbuf[slot], preferred_element_type=f32)
+
+    def refill(i, slot):
+        nxt = i + slots
+        @pl.when(nxt < nq)
+        def _():
+            weight_dyn(w_qkv, nxt, slot).start()
+        @pl.when(nxt == nq)
+        def _():
+            for j in range(rows // 8):
+                kv(k_in, kbuf, j).start()
+                kv(v_in, vbuf, j).start()
+        @pl.when(jnp.logical_and(nxt >= nq, nxt < nq + nproj))
+        def _():
+            weight_dyn(w_proj, nxt - nq, slot).start()
+
+    def query_block(j, carry):
+        slot = lax.rem(j, slots)
+        weight_dyn(w_qkv, j, slot).wait()
+        acc = project(normed, slot) + b_ref[:, pl.ds(pl.multiple_of(j * ncol, ncol), ncol)].astype(f32)
+        for i in range(per):
+            qs[pl.ds(j * per + i, rows, stride=heads), :] = rotate(acc[:, i * HEAD_DIM:(i + 1) * HEAD_DIM])
+        refill(j, slot)
+        return carry
+
+    lax.fori_loop(0, nq - 1, query_block, 0)
+
+    last = nq - 1
+    weight(last, last % slots).wait()
+    acc = project(normed, last % slots) + b_ref[:, pl.ds(last * ncol, ncol)].astype(f32)
+    refill(last, last % slots)
+    for i in range(4):
+        vals = acc[:, i * HEAD_DIM:(i + 1) * HEAD_DIM]
+        new[i] = rotate(vals) if i < 2 else vals
+
+    for j in range(rows // 8):
+        kv(k_in, kbuf, j).wait()
+        kv(v_in, vbuf, j).wait()
+
+    def insert(b, carry):
+        length = len_ref[b]
+        base = pl.multiple_of(length // 8 * 16, 16)
+        at = 2 * length - base
+        r16 = lax.broadcasted_iota(jnp.int32, (16, HEAD_DIM), 0)
+        for i, buf in ((0, kbuf), (2, vbuf)):
+            tile = buf[b, pl.ds(base, 16), :].astype(f32)
+            tile = jnp.where(r16 == at, new[i, pl.ds(b, 1), :], tile)
+            tile = jnp.where(r16 == at + 1, new[i + 1, pl.ds(b, 1), :], tile)
+            buf[b, pl.ds(base, 16), :] = tile.astype(bf16)
+        return carry
+
+    lax.fori_loop(0, rows, insert, 0)
+
+    def out_copy(b, i):
+        src, dst = ((kbuf, k_out), (vbuf, v_out))[i]
+        return pltpu.make_async_copy(src.at[pl.ds(b * nseq, nseq)], dst.at[pl.ds(b * nseq, nseq)], out_sem.at[i])
+
+    srow = lax.broadcasted_iota(jnp.int32, (heads, cache), 0)
+    scol = lax.broadcasted_iota(jnp.int32, (heads, cache), 1)
+    same_group = (srow // (heads // 2)) == (scol % 2)
+    spos = jnp.where(same_group, scol // 2, cache)
+
+    def attend(step, carry):
+        for i in range(nseq):
+            b = step * nseq + i
+            q = qs[pl.ds(pl.multiple_of(b * heads, heads), heads), :].astype(bf16)
+            s = lax.dot_general(q, kbuf[b], (((1,), (1,)), ((), ())), preferred_element_type=f32) * HEAD_DIM ** -0.5
+            s = jnp.where(spos <= len_ref[b], s, -jnp.inf)
+            e = jnp.exp(s - jnp.max(s, axis=-1, keepdims=True))
+            p = (e * (1.0 / jnp.sum(e, axis=-1, keepdims=True))).astype(bf16)
+            cs[pl.ds(pl.multiple_of(b * heads, heads), heads), :] = jnp.dot(p, vbuf[b], preferred_element_type=f32)
+        for i in range(2):
+            out_copy(step, i).start()
+        return carry
+
+    lax.fori_loop(0, rows // nseq, attend, 0)
+
+    for i in range(heads):
+        ctx[:, i * HEAD_DIM:(i + 1) * HEAD_DIM] = cs[pl.ds(i, rows, stride=heads), :].astype(bf16)
+
+    def proj_block(j, carry):
+        slot = lax.rem(j + nq, slots)
+        cols = pl.ds(pl.multiple_of(j * ncol, ncol), ncol)
+        weight_dyn(w_proj, j, slot).wait()
+        h_out[:, cols] = x_ref[:, cols].astype(f32) + project(ctx, slot)
+        refill(j + nq, slot)
+        return carry
+
+    lax.fori_loop(0, nproj, proj_block, 0)
+    m_out[...] = normalize(h_out[...], gm_ref[...].astype(f32))
+
+    def drain(step, carry):
+        for i in range(2):
+            out_copy(step, i).wait()
+        return carry
+
+    lax.fori_loop(0, rows // nseq, drain, 0)
+
+
+def attention_layer(x_in, seq_len, k_cache, v_cache, gamma_attn, w_qkv, b_qkv, w_proj, gamma_mlp):
+    rows, width = x_in.shape
+    cache_len, kv_heads = k_cache.shape[1], k_cache.shape[2]
+    heads = w_proj.shape[0] // HEAD_DIM
+    ncol, slots = 512, 6
+    f32, bf16 = jnp.float32, jnp.bfloat16
+    flat = (rows, cache_len * kv_heads, HEAD_DIM)
+    vmem = pl.BlockSpec(memory_space=pltpu.VMEM)
+    smem = pl.BlockSpec(memory_space=pltpu.SMEM)
+    hbm = pl.BlockSpec(memory_space=pl.ANY)
+    dma = pltpu.SemaphoreType.DMA
+    hidden, mlp_in, k_out, v_out = pl.pallas_call(
+        attn_kernel,
+        name='attention',
+        out_shape=(jax.ShapeDtypeStruct((rows, width), f32), jax.ShapeDtypeStruct((rows, width), bf16),
+                   jax.ShapeDtypeStruct(flat, bf16), jax.ShapeDtypeStruct(flat, bf16)),
+        in_specs=[smem, vmem, vmem, vmem, vmem, hbm, hbm, hbm, hbm],
+        out_specs=(vmem, vmem, hbm, hbm),
+        scratch_shapes=[
+            pltpu.VMEM((slots, width, ncol), bf16),
+            pltpu.VMEM(flat, bf16), pltpu.VMEM(flat, bf16),
+            pltpu.VMEM((rows, width), bf16),
+            pltpu.VMEM((rows * heads, HEAD_DIM), f32), pltpu.VMEM((rows * heads, HEAD_DIM), f32),
+            pltpu.VMEM((rows, heads * HEAD_DIM), bf16),
+            pltpu.VMEM((2 * kv_heads, rows, HEAD_DIM), f32),
+            dma((slots,)), dma((rows // 8,)), dma((2,)),
+        ],
+        compiler_params=pltpu.CompilerParams(vmem_limit_bytes=56 * 1024 * 1024),
+    )(seq_len, x_in, gamma_attn.reshape(1, -1), b_qkv.reshape(1, -1), gamma_mlp.reshape(1, -1), w_qkv, w_proj,
+      k_cache.reshape(flat), v_cache.reshape(flat))
+    return hidden, mlp_in, k_out.reshape(k_cache.shape), v_out.reshape(v_cache.shape)
 
 
 def mlp_kernel(chips, m_ref, h_ref, w_in_ref, w_out_ref, o_ref, m_all, w1, w2, act, part, pair_rx, rs_rx, rs_tx,
@@ -296,8 +436,8 @@
     repl_spec = P()
 
     def local_layer(x_in, seq_len, k_cache, v_cache, gamma_attn, w_qkv, b_qkv, w_proj, gamma_mlp, w_in, w_out):
-        hidden, k_out, v_out = attention_block(x_in, seq_len, k_cache, v_cache, gamma_attn, w_qkv, b_qkv, w_proj)
-        mlp_in = rms_norm(hidden, gamma_mlp)
+        hidden, mlp_in, k_out, v_out = attention_layer(x_in, seq_len, k_cache, v_cache, gamma_attn, w_qkv, b_qkv, w_proj,
+                                                       gamma_mlp)
         layer_out = mlp_layer(mesh, hidden, mlp_in, w_in, w_out)
         return layer_out, k_out, v_out
 

time: 136 us -> 117 us (0.86)
  Pallas kernels: 75.1 us -> 111 us
  matrix products: 35.5 us -> 0 us
  other arithmetic: 20.1 us -> 0 us
    pallas_call x0 -> x1, Pallas kernels: none -> 35.7 us  [attention_layer(): pl.pallas_call(attn_kernel, name='attention', out_shape=(jax.ShapeDtypeSt...]
    dot_general x3 -> x0, matrix products: 31.9 us -> none  [the longest x1 15.2 us: attention_block(): jnp.dot(normed, w_qkv, preferred_element_type=jnp.float32)]
    select_n x1 -> x0, other arithmetic: 13.7 us -> none  [attention_block(): k_out = jnp.where(at_len, key_new[:, None], k_cache)]
    reshape x1 -> x3, local copies, waits for them, and re-layouts: 0.02 us -> 3.92 us  [the longest x1 1.31 us: attention_layer(): b_qkv.reshape(1, -1)]
    convert_element_type x5 -> x0, other arithmetic: 3.64 us -> none  [the longest x2 1.41 us: rms_norm(): gain.astype(jnp.float32)]
    sub x1 -> x0, matrix products: 3.62 us -> none  [attention_block(): jax.nn.softmax(jnp.where(visible, attn_scores, -jnp.inf), axis=-1)]
    unnamed x9 -> x1, local copies, waits for them, and re-layouts: 2.74 us -> 1.67 us
where the time goes in v2:
time: 117 us
  Pallas kernels  111 us (95%)
  local copies, waits for them, and re-layouts  5.59 us (5%)
    pallas_call x1, Pallas kernels, mlp_layer(): pl.pallas_call(functools.partial(mlp_kernel, chips), name='mlp_ring', out...  75.1 us
    pallas_call x1, Pallas kernels, attention_layer(): pl.pallas_call(attn_kernel, name='attention', out_shape=(jax.ShapeDtypeSt...  35.7 us

profile of v2, /device:TPU:22, one launch (start us, length us, event | category | flops | bytes accessed | tf_op | source)
XLA Modules:
  0.0 117.1 jit_solution(5395325563948934819)
XLA Ops:
  0.6 1.3 %reshape.27.ga_ref = bf16[1,4096]{1,0:T(2,128)(2,1)} reshape(bf16[4096]{0:T(1024)(128)(2,1)} %param.15) | data formatting | bytes 16384 | tf_op jit(solution)/shard_map/reshape | solution.py:195
  1.9 1.3 %reshape.29.gm_ref = bf16[1,4096]{1,0:T(2,128)(2,1)} reshape(bf16[4096]{0:T(1024)(128)(2,1)} %param.19) | data formatting | bytes 16384 | tf_op jit(solution)/shard_map/reshape | solution.py:195
  3.2 1.3 %reshape.28.b_ref = bf16[1,4608]{1,0:T(2,128)(2,1)} reshape(bf16[4608]{0:T(1024)(128)(2,1)} %param.17) | data formatting | bytes 18432 | tf_op jit(solution)/shard_map/reshape | solution.py:195
  4.6 35.7 %attention.1 = (f32[32,4096]{1,0:T(8,128)}, bf16[32,4096]{1,0:T(8,128)(2,1)}, bf16[32,512,128]{2,1,0:T(8,128)(2,1)}, bf16[32,512,128]{2,1,0:T(8,128)(2,1)}) custom-call(s32[32]{0:T(128)} %len_ref.1, bf16[32,4096]{1,0:T(8,128)(2,1)} %x_ref.1, bf16[1,4096]{1,0:T(2,128)(2,1)} %reshape.27.ga_ref, bf16[1,4608]{1,0:T(2,128)(2,1)} %reshape.28.b_ref, ...), custom_call_target="tpu_custom_call" | custom-call | tf_op jit(solution)/shard_map/attention/pallas_call | solution.py:178
  40.3 75.1 %mlp_ring.1 = bf16[32,4096]{1,0:T(8,128)(2,1)} custom-call(bf16[32,4096]{1,0:T(8,128)(2,1)} %get-tuple-element.7.m_ref, f32[32,4096]{1,0:T(8,128)} %get-tuple-element.8.h_ref, bf16[2,856,4096]{2,1,0:T(8,128)(2,1)} %w_in_ref.1, bf16[856,4096]{1,0:T(8,128)(2,1)} %w_out_ref.1), custom_call_target="tpu_custom_call" | custom-call | tf_op jit(solution)/shard_map/mlp_ring/pallas_call | solution.py:409
  115.4 1.7 %copy.15 = bf16[32,4096]{1,0:T(8,128)(2,1)} copy(bf16[32,4096]{1,0:T(8,128)(2,1)} %mlp_ring.1) | data formatting | bytes 524288
